TPU v7x, 128 devices: a whole 4x4x4 slice. The times are simulated.
128 devices in a mesh: seq: 16 (over z, y_hi, core), span: 8 (over x, y_lo).
Axes of the slice: x: 4, y: 4 (y_hi: 2, y_lo: 2; y = y_hi * 2 + y_lo), z: 4, core: 2. Of those that a mesh axis runs over, the one named last changes fastest.
Arguments:
- q_prefill: bfloat16 [8, 2048, 64, 192], P('span', 'seq'), may hold values from -3000 to 3000
- kv_latent: bfloat16 [8, 2048, 512], P('span', 'seq'), may hold values from -200 to 200
- key_rope: bfloat16 [8, 2048, 64], P('span', 'seq'), may hold values from -6 to 6
- segment_ids: int32 [8, 2048], replicated, may hold values from 0 to 15, never falling along the last dimension, each value on 1 to 1024 neighbouring positions
- assignment: int32 [128], replicated, may hold values from 0 to 127, each once
- absorb_key: bfloat16 [64, 128, 512], replicated, may hold values from -0.5 to 0.5
- absorb_value: bfloat16 [64, 512, 128], replicated, may hold values from -0.25 to 0.25
- q_decode: bfloat16 [2, 128, 64, 192], P(None, 'span'), may hold values from -3000 to 3000
- new_latent: bfloat16 [2, 128, 512], P(None, 'span'), may hold values from -6 to 6
- new_rope: bfloat16 [2, 128, 64], P(None, 'span'), may hold values from -6 to 6
Outputs:
- prefill_out: bfloat16 [8, 2048, 8192], P('span', 'seq')
- decode_out: bfloat16 [2, 128, 8192], P(None, 'span')
Inputs may be any that keep to these rules, and one draw needn't show every extreme that they name: `segment_ids`: within a span the numbers never fall; each of the 16 numbers appears, on 1 to 1024 positions. `assignment`: each sequence number appears once; entry c * 16 + d is the sequence of prompt d of span c, and sequence g is decoded at span index g // 16, slot g % 16.
All inputs are finite; a program needn't handle non-finite values.
Results may differ from a plain program's by a relative error of at most 0.014.
Values may be sent and summed in bfloat16 or wider, within the bound.
A program may use at most 192 MiB of HBM per device.

v0:
```python
import math

import jax
import jax.numpy as jnp
from jax import lax
from jax.experimental import pallas as pl
from jax.experimental.pallas import tpu as pltpu
from jax.sharding import PartitionSpec as P

H = 64
NOPE = 128
ROPE = 64
LAT = 512
VHEAD = 128
TOK = 128
DOCS = 16
STEPS = 2
NSEQ = 16
NSPAN = 8
WIDE = 640
AUG = 64
BIG = float(2.0**100)
EPS = 1e-06
SCALE = (NOPE + ROPE) ** (-0.5)
EXPC = SCALE * math.log2(math.e)
GROUP = 8
NG = H // GROUP
CH = 2
QCOL = 2048 + 2 * WIDE
BF = jnp.bfloat16
F32 = jnp.float32
MESH = pl.DeviceIdType.MESH


def cache_rows(latent, rope):
    values = latent.astype(F32)
    normed = values * lax.rsqrt(jnp.mean(values * values, axis=-1, keepdims=True) + EPS)
    return jnp.concatenate([normed, rope.astype(F32)], axis=-1).astype(BF)


def nt_dot(a, b):
    return lax.dot_general(a, b, (((1,), (1,)), ((), ())), preferred_element_type=F32)


def nn_dot(a, b):
    return jnp.dot(a, b, preferred_element_type=F32)


def kernel(
    own_ref, qm_ref, sel_ref, selo_ref, qaug_ref, daug_ref, faug_ref, tri_ref, wkd_ref, wvd_ref,
    q_ref, wk_ref, wv_ref,
    out_ref, dec_ref,
    cb, qa, qf, qr, qall, do_own, doall, so, outbuf,
    g_send, g_recv, q_send, q_recv, o_send, o_recv, s_send, s_recv,
):
    step = pl.program_id(0)
    me = lax.axis_index("seq")
    span = lax.axis_index("span")
    z = me // 4
    yh = (me // 2) % 2
    k = me % 2
    zp = (z + 1) % 4
    zm = (z + 3) % 4
    z2 = (z + 2) % 4

    def idx(zz, yy, kk):
        return zz * 4 + yy * 2 + kk

    part = idx(z, yh, 1 - k)
    ypeer = idx(z, 1 - yh, k)
    up = idx(zp, yh, k)
    down = idx(zm, yh, k)

    def rows(block, owner):
        slot = (block - owner + 24) % 16
        return cb.at[pl.ds(pl.multiple_of(slot * TOK, TOK), TOK)]

    kinds = [
        idx(z, 1 - yh, k),
        idx(zm, yh, k),
        idx(zp, yh, k),
        idx(zm, 1 - yh, k),
        idx(zp, 1 - yh, k),
        idx(z2, yh, k),
        idx(z2, 1 - yh, k),
    ]
    arrive = kinds + [part] + [b + 1 - 2 * k for b in kinds]

    def copy(src, block, target, kind, send, dst=None):
        return pltpu.make_async_remote_copy(
            src_ref=src,
            dst_ref=rows(block, target) if dst is None else dst,
            send_sem=g_send.at[send],
            recv_sem=g_recv.at[kind],
            device_id=(target, span),
            device_id_type=MESH,
        )

    plan = [
        (None, me, ypeer, 0),
        (None, me, up, 1),
        (None, me, part, 7),
        (None, me, down, 2),
        (0, kinds[0], up, 3),
        (0, kinds[0], down, 4),
        (0, kinds[0], part, 8),
        (1, kinds[1], up, 5),
        (1, kinds[1], part, 9),
        (3, kinds[3], part, 11),
        (4, kinds[4], down, 6),
        (4, kinds[4], part, 12),
        (2, kinds[2], part, 10),
        (5, kinds[5], part, 13),
        (6, kinds[6], part, 14),
    ]

    def send(i):
        source, block, target, kind = plan[i]
        src = own_ref if source is None else rows(block, me)
        return copy(src, block, target, kind, i)

    def landed(kind):
        copy(own_ref, arrive[kind], part, kind, 0, rows(arrive[kind], me)).wait_recv()

    def q_copy(off):
        return pltpu.make_async_remote_copy(
            src_ref=qm_ref,
            dst_ref=qall.at[pl.ds(pl.multiple_of(span * DOCS, DOCS), DOCS)],
            send_sem=q_send.at[off - 1],
            recv_sem=q_recv.at[off - 1],
            device_id=(me, (span + off) % NSPAN),
            device_id_type=MESH,
        )

    def o_copy(off):
        return pltpu.make_async_remote_copy(
            src_ref=do_own,
            dst_ref=doall.at[span],
            send_sem=o_send.at[off - 1],
            recv_sem=o_recv.at[off - 1],
            device_id=(me, (span + off) % NSPAN),
            device_id_type=MESH,
        )

    def s_copy(off):
        return pltpu.make_async_remote_copy(
            src_ref=so,
            dst_ref=outbuf.at[:, :, pl.ds(pl.multiple_of(me * 512, 512), 512)],
            send_sem=s_send.at[off - 1],
            recv_sem=s_recv.at[off - 1],
            device_id=((me + off) % NSEQ, span),
            device_id_type=MESH,
        )

    @pl.when(step == 0)
    def _():
        barrier = pltpu.get_barrier_semaphore()
        for off in range(1, NSEQ):
            pl.semaphore_signal(
                barrier, inc=1, device_id=((me + off) % NSEQ, span), device_id_type=MESH
            )
        for off in range(1, NSPAN):
            pl.semaphore_signal(
                barrier, inc=1, device_id=(me, (span + off) % NSPAN), device_id_type=MESH
            )
        pl.semaphore_wait(barrier, NSEQ + NSPAN - 2)
        for i in range(4):
            send(i).start()
        for off in (1, 7, 2, 6, 3, 5, 4):
            q_copy(off).start()
        cb[pl.ds(8 * TOK, TOK), :] = own_ref[...]
        qall[pl.ds(pl.multiple_of(span * DOCS, DOCS), DOCS), :] = qm_ref[...]

    @pl.when(step < NG)
    def _():
        block = q_ref[...].astype(F32).reshape(TOK * GROUP, NOPE + ROPE)
        qf[...] = block[:, 0:NOPE]
        qr[:, 0:ROPE] = block[:, NOPE:]
        for j in range(GROUP):
            nope = qf[pl.ds(j, TOK, stride=GROUP), :].astype(BF)
            rope = qr[pl.ds(j, TOK, stride=GROUP), :][:, 0:ROPE].astype(BF)
            at = pl.ds(pl.multiple_of((step * GROUP + j) * TOK, TOK), TOK)
            qa[at, 0:LAT] = nn_dot(nope, wk_ref[j]).astype(BF)
            qa[at, LAT:WIDE] = jnp.concatenate([rope, qaug_ref[...]], axis=1)

    @pl.when(step == NG)
    def _():
        landed(1)
        send(7).start()
        send(8).start()
        landed(0)
        for i in (4, 5, 6):
            send(i).start()
        landed(3)
        send(9).start()
        landed(4)
        send(10).start()
        send(11).start()
        landed(2)
        send(12).start()
        landed(5)
        send(13).start()
        landed(6)
        send(14).start()
        for kind in range(7, 15):
            landed(kind)
        for i in range(15):
            send(i).wait_send()

    @pl.when(step >= NG)
    def _():
        base = (step - NG) * GROUP * TOK
        keys = cb[pl.ds(0, 9 * TOK), :]
        vals = cb[pl.ds(0, 9 * TOK), pl.ds(0, LAT)]
        tri = jnp.concatenate([tri_ref[...]] * CH, axis=0)
        count = GROUP // CH

        def score(n):
            at = pl.ds(pl.multiple_of(base + n * CH * TOK, CH * TOK), CH * TOK)
            return nt_dot(qa[at, :], keys)

        s_next = score(0)
        for n in range(count):
            s = s_next
            if n + 1 < count:
                s_next = score(n + 1)
            s = jnp.concatenate([s[:, : 8 * TOK], s[:, 8 * TOK :] + tri], axis=1)
            best = jnp.max(s, axis=1, keepdims=True)
            w = jnp.exp2((s - best) * EXPC)
            total = jnp.sum(w, axis=1, keepdims=True)
            o = (nn_dot(w.astype(BF), vals) / total).astype(BF)
            for j in range(CH):
                h = n * CH + j
                out_ref[:, h * VHEAD : (h + 1) * VHEAD] = nn_dot(
                    o[j * TOK : (j + 1) * TOK], wv_ref[h]
                ).astype(BF)

    @pl.when(step == NG + 1)
    def _():
        for off in range(1, NSPAN):
            q_copy(off).wait()
        chosen = nn_dot(sel_ref[...], qall[...]).astype(BF)
        fresh = [
            chosen[:, 2048 + u * WIDE : 2048 + (u + 1) * WIDE] + faug_ref[pl.ds(u * DOCS, DOCS), :]
            for u in range(STEPS)
        ]
        cb[pl.ds(16 * TOK, TOK), :] = jnp.concatenate(
            fresh + [faug_ref[pl.ds(STEPS * DOCS, TOK - STEPS * DOCS), :]], axis=0
        )
        parts = []
        for j in range(4):
            nope = jnp.concatenate(
                [chosen[:, (j * 2 + t) * 256 : (j * 2 + t) * 256 + 128] for t in range(STEPS)], axis=0
            )
            rope = jnp.concatenate(
                [chosen[:, (j * 2 + t) * 256 + 128 : (j * 2 + t + 1) * 256] for t in range(STEPS)],
                axis=0,
            )
            lat = nn_dot(nope, wkd_ref[j]).astype(BF)
            parts.append(jnp.concatenate([lat, rope + daug_ref[...]], axis=1))
        dq = jnp.concatenate(parts, axis=0)
        s = nt_dot(dq, cb[...])
        best = jnp.max(s, axis=1, keepdims=True)
        w = jnp.exp2((s - best) * EXPC)
        total = jnp.sum(w, axis=1, keepdims=True)
        acc = nn_dot(w.astype(BF), cb[:, pl.ds(0, LAT)])
        for j in range(4):
            rest = acc[j * 32 : (j + 1) * 32]
            split = []
            for _ in range(3):
                piece = rest.astype(BF)
                split.append(piece)
                rest = rest - piece.astype(F32)
            y = nn_dot(jnp.concatenate(split, axis=0), wvd_ref[j])
            y = (y[0:32] + y[32:64] + y[64:96]) / total[j * 32 : (j + 1) * 32]
            y = y.astype(BF)
            for t in range(STEPS):
                do_own[t, :, j * VHEAD : (j + 1) * VHEAD] = y[t * DOCS : (t + 1) * DOCS]

    @pl.when(step == NG + 2)
    def _():
        for off in (1, 7, 2, 6, 3, 5, 4):
            o_copy(off).start()
        doall[span] = do_own[...]

    @pl.when(step == NG + 4)
    def _():
        for off in range(1, NSPAN):
            o_copy(off).wait()
        for t in range(STEPS):
            full = jnp.concatenate([doall[i, t] for i in range(NSPAN)], axis=0)
            so[t] = nn_dot(selo_ref[...], full).astype(BF)

    @pl.when(step == NG + 5)
    def _():
        for off in range(1, NSEQ):
            s_copy(off).start()
        outbuf[:, :, pl.ds(pl.multiple_of(me * 512, 512), 512)] = so[...]

    @pl.when(step == 2 * NG - 1)
    def _():
        for off in range(1, NSEQ):
            s_copy(off).wait()
        dec_ref[...] = outbuf[...]


def body(
    q_prefill, kv_latent, key_rope, segment_ids, assignment, absorb_key, absorb_value,
    q_decode, new_latent, new_rope,
):
    me = lax.axis_index("seq")
    span = lax.axis_index("span")
    seg = lax.dynamic_slice(segment_ids, (span, me * TOK), (1, TOK))[0]
    numbers = jnp.arange(DOCS, dtype=jnp.int32)
    same = seg[:, None] == numbers[None, :]
    here = jnp.broadcast_to((numbers == me)[None, :], (TOK, NSEQ))
    zeros32 = jnp.zeros((TOK, AUG - 32), F32)
    own_aug = jnp.concatenate([same.astype(F32), here.astype(F32), zeros32], axis=1).astype(BF)
    own = jnp.concatenate([cache_rows(kv_latent[0], key_rope[0]), own_aug], axis=1)
    later = jnp.broadcast_to((numbers > me)[None, :], (TOK, NSEQ))
    qaug = jnp.concatenate(
        [jnp.where(same, 0.0, -BIG), jnp.where(later, -BIG, 0.0), zeros32], axis=1
    ).astype(BF)

    mine = lax.dynamic_slice(q_decode, (0, 0, me * 4, 0), (STEPS, DOCS, 4, NOPE + ROPE))
    mine = jnp.pad(mine, ((0, 0), (0, 0), (0, 0), (0, 64))).transpose(1, 2, 0, 3).reshape(DOCS, 2048)
    fresh = jnp.pad(cache_rows(new_latent, new_rope), ((0, 0), (0, 0), (0, AUG)))
    qm = jnp.concatenate([mine, fresh[0], fresh[1]], axis=1)

    every = jnp.arange(NSPAN * DOCS, dtype=jnp.int32)
    own_docs = lax.dynamic_slice(assignment, (span * DOCS,), (DOCS,))
    sel = (own_docs[:, None] == every[None, :]).astype(BF)
    selo = (assignment[None, :] == (span * DOCS + numbers)[:, None]).astype(BF)

    row = jnp.arange(STEPS * DOCS, dtype=jnp.int32)
    col = jnp.arange(128, dtype=jnp.int32) - ROPE
    not_doc = (col[None, :] >= 0) & (col[None, :] < 16) & (col[None, :] != (row % DOCS)[:, None])
    not_step = (col[None, :] == 32) & ((row // DOCS)[:, None] == 0)
    daug = jnp.where(not_doc | not_step | (col == 33)[None, :], -BIG, 0.0).astype(BF)
    frow = jnp.arange(TOK, dtype=jnp.int32)
    fcol = jnp.arange(WIDE, dtype=jnp.int32) - LAT - ROPE
    real = (frow < STEPS * DOCS)[:, None]
    fdoc = real & (fcol[None, :] >= 0) & (fcol[None, :] < 16) & (fcol[None, :] == (frow % DOCS)[:, None])
    fstep = real & (fcol == 32)[None, :] & ((frow // DOCS) == 1)[:, None]
    fpad = (~real) & (fcol == 33)[None, :]
    faug = (fdoc | fstep | fpad).astype(BF)
    tri = jnp.where(frow[:, None] >= frow[None, :], 0.0, -1e30).astype(F32)

    wkd = lax.dynamic_slice(absorb_key, (me * 4, 0, 0), (4, NOPE, LAT))
    wvd = lax.dynamic_slice(absorb_value, (me * 4, 0, 0), (4, LAT, VHEAD))

    vmem = pl.BlockSpec(memory_space=pltpu.VMEM)
    out, dec = pl.pallas_call(
        kernel,
        grid=(2 * NG,),
        out_shape=(
            jax.ShapeDtypeStruct((TOK, H * VHEAD), BF),
            jax.ShapeDtypeStruct((STEPS, DOCS, H * VHEAD), BF),
        ),
        in_specs=[vmem] * 10
        + [
            pl.BlockSpec((TOK, GROUP, NOPE + ROPE), lambda i: (0, jnp.minimum(i, NG - 1), 0)),
            pl.BlockSpec((GROUP, NOPE, LAT), lambda i: (jnp.minimum(i, NG - 1), 0, 0)),
            pl.BlockSpec((GROUP, LAT, VHEAD), lambda i: (jnp.maximum(i - NG, 0), 0, 0)),
        ],
        out_specs=(
            pl.BlockSpec((TOK, GROUP * VHEAD), lambda i: (0, jnp.maximum(i - NG, 0))),
            pl.BlockSpec((STEPS, DOCS, H * VHEAD), lambda i: (0, 0, 0)),
        ),
        scratch_shapes=[
            pltpu.VMEM((17 * TOK, WIDE), BF),
            pltpu.VMEM((H * TOK, WIDE), BF),
            pltpu.VMEM((TOK * GROUP, NOPE), F32),
            pltpu.VMEM((TOK * GROUP, NOPE), F32),
            pltpu.VMEM((NSPAN * DOCS, QCOL), BF),
            pltpu.VMEM((STEPS, DOCS, 512), BF),
            pltpu.VMEM((NSPAN, STEPS, DOCS, 512), BF),
            pltpu.VMEM((STEPS, DOCS, 512), BF),
            pltpu.VMEM((STEPS, DOCS, H * VHEAD), BF),
            pltpu.SemaphoreType.DMA((15,)),
            pltpu.SemaphoreType.DMA((15,)),
            pltpu.SemaphoreType.DMA((7,)),
            pltpu.SemaphoreType.DMA((7,)),
            pltpu.SemaphoreType.DMA((7,)),
            pltpu.SemaphoreType.DMA((7,)),
            pltpu.SemaphoreType.DMA((15,)),
            pltpu.SemaphoreType.DMA((15,)),
        ],
        compiler_params=pltpu.CompilerParams(
            dimension_semantics=("arbitrary",),
            collective_id=0,
            has_side_effects=True,
            vmem_limit_bytes=60 * 1024 * 1024,
        ),
    )(
        own, qm, sel, selo, qaug, daug, faug, tri, wkd, wvd,
        q_prefill[0], absorb_key, absorb_value,
    )
    return (out[None], dec)


def solution(mesh):
    in_specs = (
        P("span", "seq", None, None),
        P("span", "seq", None),
        P("span", "seq", None),
        P(),
        P(),
        P(),
        P(),
        P(None, "span", None, None),
        P(None, "span", None),
        P(None, "span", None),
    )
    out_specs = (P("span", "seq", None), P(None, "span", None))
    return jax.shard_map(body, mesh=mesh, in_specs=in_specs, out_specs=out_specs, check_vma=False)
```

profile of v0, /device:TPU:1, one launch (start us, length us, event | category | flops | bytes accessed | tf_op | source)
XLA Modules:
  0.0 103.9 jit_solution(15518894479480830761)
XLA Ops:
  0.6 0.0 copy-start
  0.7 0.8 dynamic_slice.17
  1.5 0.8 dynamic-slice_bitcast_fusion
  2.2 1.0 fusion
  3.3 0.1 pad.11.clone
  3.4 0.8 fusion.4
  4.3 0.7 select_convert_fusion.1.daug_ref
  5.0 1.3 %fusion.8 = (bf16[16,128]{1,0:T(8,128)(2,1)}, bf16[16,128]{1,0:T(8,128)(2,1)}) fusion(s32[16]{0:T(128)S(1)} %dynamic_slice.17, s32[16]{0:T(128)S(1)} %iota_add_fusion.2, s32[128]{0:T(128)} %param.14), kind=kLoop, calls=%fused_computation.25 | loop fusion | flops 8192 | bytes 8832 | tf_op jit(solution)/shard_map/convert_element_type | solution.py:332
  6.3 0.8 fusion.5
  7.1 0.7 fusion.7
  7.9 0.8 copy.12
  8.7 0.1 select_convert_fusion
  8.8 0.7 pad_maximum_fusion.1.qaug_ref
  9.5 0.1 convert_convert_fusion
  9.6 0.0 copy-done
  9.7 0.1 copy.13
  9.8 0.7 pad_maximum_fusion.qm_ref
  10.5 0.6 fusion.6.tri_ref
  11.1 1.0 fusion.1
  12.1 0.8 concatenate.19.own_ref
  12.9 0.9 or_convert_fusion.faug_ref
  13.8 1.9 %constant_dynamic-slice_fusion.1.wkd_ref = bf16[4,128,512]{2,1,0:T(8,128)(2,1)} fusion(bf16[64,128,512]{2,1,0:T(8,128)(2,1)} %wk_ref.1, s32[]{:T(128)S(6)} %select_n.71), kind=kLoop, calls=%fused_computation.45 | loop fusion | bytes 1048580 | tf_op jit(solution)/shard_map/dynamic_slice | solution.py:349
  15.6 1.9 %constant_dynamic-slice_fusion.wvd_ref = bf16[4,512,128]{2,1,0:T(8,128)(2,1)} fusion(bf16[64,512,128]{2,1,0:T(8,128)(2,1)} %wv_ref.1, s32[]{:T(128)S(6)} %select_n.71), kind=kLoop, calls=%fused_computation.44 | loop fusion | bytes 1048580 | tf_op jit(solution)/shard_map/dynamic_slice | solution.py:350
  17.5 6.7 %copy.14 = bf16[1,128,64,192]{3,2,1,0:T(8,128)(2,1)} copy(bf16[1,128,64,192]{1,3,2,0:T(8,128)(2,1)} %param.10) | data formatting | bytes 6291456 | tf_op args[0]
  24.2 74.7 %shard_map.113 = (bf16[128,8192]{1,0:T(8,128)(2,1)}, bf16[2,16,8192]{2,1,0:T(8,128)(2,1)}) custom-call(bf16[128,640]{1,0:T(8,128)(2,1)} %concatenate.19.own_ref, bf16[16,3328]{1,0:T(8,128)(2,1)} %pad_maximum_fusion.qm_ref, bf16[16,128]{1,0:T(8,128)(2,1)} %get-tuple-element.18.sel_ref, bf16[16,128]{1,0:T(8,128)(2,1)} %get-tuple-element.19.selo_ref, ...), custom_call_target="tpu_custom_call" | custom-call | tf_op jit(solution)/shard_map/pallas_call | solution.py:353
  99.0 3.1 %copy.17 = bf16[1,128,8192]{2,1,0:T(8,128)(2,1)} copy(bf16[1,128,8192]{2,1,0:T(8,128)(2,1)} %bitcast.16) | data formatting | bytes 4194304
  102.1 1.9 %copy.18 = bf16[2,16,8192]{2,1,0:T(8,128)(2,1)} copy(bf16[2,16,8192]{2,1,0:T(8,128)(2,1)} %get-tuple-element.23) | data formatting | bytes 1048576
  (21 shorter events, 0.2 us)
Async XLA Ops:
  0.6 9.0 %copy-start = (bf16[2,16,64,192]{3,2,1,0:T(8,128)(2,1)S(1)}, bf16[2,16,64,192]{3,2,1,0:T(8,128)(2,1)}, u32[]{:S(2)}) copy-start(bf16[2,16,64,192]{3,2,1,0:T(8,128)(2,1)} %param.17) | copy-start | bytes 2359300
where the time goes:
time: 105 us; the launch traced here: 104 us
  Pallas kernels  74.7 us (71%)
  local copies, waits for them, and re-layouts  18.9 us (18%)
  other arithmetic  9.49 us (9%)
    pallas_call x1, Pallas kernels, body(): pl.pallas_call(kernel, grid=(2 * NG,), out_shape=(jax.ShapeDtypeStruct((T...  74.7 us
    unnamed x6, local copies, waits for them, and re-layouts  12.5 us

commit v1 on v0

v1 whole, which is shorter than its diff:
```python
import math

import jax
import jax.numpy as jnp
from jax import lax
from jax.experimental import pallas as pl
from jax.experimental.pallas import tpu as pltpu
from jax.sharding import PartitionSpec as P

H = 64
NOPE = 128
ROPE = 64
LAT = 512
VHEAD = 128
TOK = 128
DOCS = 16
STEPS = 2
NSEQ = 16
NSPAN = 8
WIDE = 640
AUG = 64
BIG = float(2.0**100)
EPS = 1e-06
SCALE = (NOPE + ROPE) ** (-0.5)
EXPC = SCALE * math.log2(math.e)
GROUP = 8
NG = H // GROUP
CH = 2
RELAY0 = 4
RELAY1 = 6
DEC = NG + 2
QCOL = 2688
FRESH = 1536
BF = jnp.bfloat16
F32 = jnp.float32
MESH = pl.DeviceIdType.MESH


def normed(values):
    values = values.astype(F32)
    mean = jnp.mean(values * values, axis=-1, keepdims=True)
    return values * lax.rsqrt(mean + EPS)


def iota(shape, dim):
    return lax.broadcasted_iota(jnp.int32, shape, dim)


def nt_dot(a, b):
    return lax.dot_general(a, b, (((1,), (1,)), ((), ())), preferred_element_type=F32)


def nn_dot(a, b):
    return jnp.dot(a, b, preferred_element_type=F32)


def kernel(
    lat_ref, rope_ref, seg_ref, assign_ref, qd_ref, nl_ref, nr_ref, wk_any, wv_any,
    q_ref, wk_ref, wv_ref,
    out_ref, dec_ref,
    cb, qa, s1, qaug, qf, qr, qm, qall, selbuf, wkd, wvd, do_own, doall, so, outbuf,
    g_send, g_recv, q_send, q_recv, o_send, o_recv, s_send, s_recv, w_sem,
):
    step = pl.program_id(0)
    me = lax.axis_index("seq")
    span = lax.axis_index("span")
    z = me // 4
    yh = (me // 2) % 2
    k = me % 2
    zp = (z + 1) % 4
    zm = (z + 3) % 4
    z2 = (z + 2) % 4

    def idx(zz, yy, kk):
        return zz * 4 + yy * 2 + kk

    part = idx(z, yh, 1 - k)
    ypeer = idx(z, 1 - yh, k)
    up = idx(zp, yh, k)
    down = idx(zm, yh, k)

    def rows(block, owner):
        slot = (block - owner + 24) % 16
        return cb.at[pl.ds(pl.multiple_of(slot * TOK, TOK), TOK)]

    kinds = [
        idx(z, 1 - yh, k),
        idx(zm, yh, k),
        idx(zp, yh, k),
        idx(zm, 1 - yh, k),
        idx(zp, 1 - yh, k),
        idx(z2, yh, k),
        idx(z2, 1 - yh, k),
    ]
    arrive = kinds + [part] + [b + 1 - 2 * k for b in kinds]

    def copy(src, dst, target, kind, number):
        return pltpu.make_async_remote_copy(
            src_ref=src,
            dst_ref=dst,
            send_sem=g_send.at[number],
            recv_sem=g_recv.at[kind],
            device_id=(target, span),
            device_id_type=MESH,
        )

    plan = [
        (me, ypeer, 0),
        (me, up, 1),
        (me, part, 7),
        (me, down, 2),
        (kinds[0], up, 3),
        (kinds[0], down, 4),
        (kinds[0], part, 8),
        (kinds[1], up, 5),
        (kinds[1], part, 9),
        (kinds[3], part, 11),
        (kinds[4], down, 6),
        (kinds[4], part, 12),
        (kinds[2], part, 10),
        (kinds[5], part, 13),
        (kinds[6], part, 14),
    ]

    def send(i):
        block, target, kind = plan[i]
        return copy(rows(block, me), rows(block, target), target, kind, i)

    def landed(kind):
        dst = rows(arrive[kind], me)
        copy(dst, dst, part, kind, 0).wait_recv()

    x = span // 2
    lo = span % 2
    lopeer = x * 2 + 1 - lo

    def qrows(src):
        return qall.at[pl.ds(pl.multiple_of(src * DOCS, DOCS), DOCS)]

    def q_copy(src, dst, target, number):
        return pltpu.make_async_remote_copy(
            src_ref=src,
            dst_ref=dst,
            send_sem=q_send.at[number],
            recv_sem=q_recv.at[number],
            device_id=(me, target),
            device_id_type=MESH,
        )

    def q_send_of(number):
        if number == 0:
            return q_copy(qm, qrows(span), lopeer, 0)
        xx = (x + (number - 1) % 3 + 1) % 4
        if number <= 3:
            return q_copy(qm, qrows(span), xx * 2 + lo, number)
        return q_copy(qrows(lopeer), qrows(lopeer), xx * 2 + lo, number)

    def q_landed(number):
        if number == 0:
            src = lopeer
        else:
            xx = (x + 3 - (number - 1) % 3) % 4
            src = xx * 2 + (lo if number <= 3 else 1 - lo)
        q_copy(qrows(src), qrows(src), lopeer, number).wait_recv()

    def o_copy(off):
        return pltpu.make_async_remote_copy(
            src_ref=do_own,
            dst_ref=doall.at[span],
            send_sem=o_send.at[off - 1],
            recv_sem=o_recv.at[off - 1],
            device_id=(me, (span + off) % NSPAN),
            device_id_type=MESH,
        )

    def columns(block):
        return outbuf.at[:, :, pl.ds(pl.multiple_of(block * 512, 512), 512)]

    def s_copy(src, dst, target, number):
        return pltpu.make_async_remote_copy(
            src_ref=src,
            dst_ref=dst,
            send_sem=s_send.at[number],
            recv_sem=s_recv.at[number],
            device_id=(target, span),
            device_id_type=MESH,
        )

    def chip(off):
        return ((me // 2 + off) % 8) * 2 + k

    def s_out(number):
        if number == 7:
            return s_copy(so, columns(me), part, 7)
        if number < 7:
            return s_copy(so, columns(me), chip(number + 1), number)
        block = chip(8 - (number - 7))
        return s_copy(columns(block), columns(block), part, number)

    def s_landed(number):
        if number == 7:
            block = part
        elif number < 7:
            block = chip(8 - (number + 1))
        else:
            block = chip(8 - (number - 7)) + 1 - 2 * k
        s_copy(columns(block), columns(block), part, number).wait_recv()

    wk_copy = lambda: pltpu.make_async_copy(wk_any.at[pl.ds(me * 4, 4)], wkd, w_sem.at[0])
    wv_copy = lambda: pltpu.make_async_copy(wv_any.at[pl.ds(me * 4, 4)], wvd, w_sem.at[1])

    @pl.when(step == 0)
    def _():
        barrier = pltpu.get_barrier_semaphore()
        for off in range(1, NSEQ):
            pl.semaphore_signal(
                barrier, inc=1, device_id=((me + off) % NSEQ, span), device_id_type=MESH
            )
        for off in range(1, NSPAN):
            pl.semaphore_signal(
                barrier, inc=1, device_id=(me, (span + off) % NSPAN), device_id_type=MESH
            )
        wk_copy().start()
        wv_copy().start()
        cb[pl.ds(8 * TOK, TOK), 0:LAT] = normed(lat_ref[...]).astype(BF)
        segs = seg_ref[:, pl.ds(pl.multiple_of(me * TOK, TOK), TOK)].astype(F32)
        seg = jnp.sum(jnp.where(iota((NSPAN, TOK), 0) == span, segs, 0.0), axis=0, keepdims=True)
        seg = seg.astype(jnp.int32)
        number = iota((AUG, TOK), 0)
        same = number == seg
        kaug = jnp.where(same | (number - 16 == me), 1.0, 0.0)
        late = (number >= 16) & (number < 32) & (number - 16 > me)
        wrong = ((number < 16) & jnp.logical_not(same)) | late
        qaug[...] = jnp.where(wrong, -BIG, 0.0).astype(BF)
        tail = jnp.concatenate([rope_ref[...].astype(F32), kaug], axis=0)
        cb[pl.ds(8 * TOK, TOK), LAT:WIDE] = tail.T.astype(BF)
        at8 = pl.ds(pl.multiple_of((me // 2) * 8, 8), 8)
        for t in range(STEPS):
            block = qd_ref[t, :, at8, :].astype(F32).reshape(DOCS * 8, NOPE + ROPE)
            qf[t] = block[:, 0:NOPE]
            qr[t, :, 0:ROPE] = block[:, NOPE:]
        for j in range(4):
            ropes = []
            for t in range(STEPS):
                pick = pl.ds(k * 4 + j, DOCS, stride=8)
                n = j * 2 + t
                qm[:, n * 128 : (n + 1) * 128] = qf.at[t][pick, :].astype(BF)
                ropes.append(qr.at[t][pick, :][:, 0:ROPE])
            qm[:, 1024 + j * 128 : 1024 + (j + 1) * 128] = jnp.concatenate(ropes, axis=1).astype(BF)
        for t in range(STEPS):
            qm[:, FRESH + t * LAT : FRESH + (t + 1) * LAT] = normed(nl_ref[t]).astype(BF)
        both = jnp.concatenate([nr_ref[0].astype(F32), nr_ref[1].astype(F32)], axis=1)
        qm[:, FRESH + 2 * LAT : QCOL] = both.astype(BF)
        pl.semaphore_wait(barrier, NSEQ + NSPAN - 2)
        for i in (1, 0, 2):
            send(i).start()
        for n in (1, 3, 2):
            q_send_of(n).start()
        qrows(span)[...] = qm[...]
        selbuf[...] = jnp.where(assign_ref[...] == iota((128, 128), 0), 1.0, 0.0).T

    @pl.when(step < NG)
    def _():
        own_keys = cb[pl.ds(8 * TOK, TOK), :]
        tri = jnp.where(iota((TOK, TOK), 0) >= iota((TOK, TOK), 1), 0.0, -1e30)
        first = pl.multiple_of(step * GROUP * TOK, GROUP * TOK)
        for j in range(GROUP):
            at = pl.ds(pl.multiple_of(first + j * TOK, TOK), TOK)
            nope = q_ref[j, 0:NOPE, :].T
            qa[at, 0:LAT] = nn_dot(nope, wk_ref[j]).astype(BF)
            qa[at, LAT:WIDE] = jnp.concatenate([q_ref[j, NOPE:, :], qaug[...]], axis=0).T
        for j in range(0, GROUP, 4):
            at = pl.ds(pl.multiple_of(first + j * TOK, 4 * TOK), 4 * TOK)
            s1[at, :] = nt_dot(qa[at, :], own_keys) + jnp.concatenate([tri] * 4, axis=0)

    @pl.when(step == RELAY0)
    def _():
        landed(1)
        send(7).start()
        send(8).start()

    @pl.when(step == RELAY1)
    def _():
        landed(0)
        for i in (4, 5, 6, 3):
            send(i).start()
        q_send_of(0).start()

    @pl.when(step == NG)
    def _():
        landed(3)
        send(9).start()
        landed(4)
        send(10).start()
        send(11).start()
        landed(5)
        send(13).start()
        landed(6)
        send(14).start()
        q_landed(0)
        for n in (4, 6, 5):
            q_send_of(n).start()
        for kind in (7, 8, 9, 11, 13, 14):
            landed(kind)

    @pl.when(step == NG + 1)
    def _():
        landed(2)
        send(12).start()

    @pl.when(step == DEC)
    def _():
        landed(10)
        landed(12)
        for i in range(15):
            send(i).wait_send()
        wk_copy().wait()
        wv_copy().wait()
        for n in range(1, 7):
            q_landed(n)
        for n in range(7):
            q_send_of(n).wait_send()
        sel = selbuf[pl.ds(pl.multiple_of(span * DOCS, DOCS), DOCS), :].astype(BF)
        chosen = nn_dot(sel, qall[...]).astype(BF)
        col = iota((DOCS, AUG), 1)
        doc = iota((DOCS, AUG), 0)
        last = FRESH + 2 * LAT
        for t in range(STEPS):
            at = pl.ds(16 * TOK + t * DOCS, DOCS)
            cb[at, 0:LAT] = chosen[:, FRESH + t * LAT : FRESH + (t + 1) * LAT]
            mark = jnp.where((col == doc) | ((col == 32) & (t == 1)), 1.0, 0.0)
            rope = chosen[:, last + t * ROPE : last + (t + 1) * ROPE].astype(F32)
            cb[at, LAT:WIDE] = jnp.concatenate([rope, mark], axis=1).astype(BF)
        pad = TOK - STEPS * DOCS
        cb[pl.ds(16 * TOK + STEPS * DOCS, pad), :] = jnp.where(
            iota((pad, WIDE), 1) == LAT + ROPE + 33, 1.0, 0.0
        ).astype(BF)
        row = iota((STEPS * DOCS, AUG), 0)
        dcol = iota((STEPS * DOCS, AUG), 1)
        wrong = ((dcol < 16) & (dcol != row % DOCS)) | ((dcol == 32) & (row < DOCS)) | (dcol == 33)
        daug = jnp.where(wrong, -BIG, 0.0)
        parts = []
        for j in range(4):
            nope = jnp.concatenate(
                [chosen[:, (j * 2 + t) * 128 : (j * 2 + t + 1) * 128] for t in range(STEPS)], axis=0
            )
            at = 1024 + j * 128
            rope = jnp.concatenate(
                [chosen[:, at + t * ROPE : at + (t + 1) * ROPE] for t in range(STEPS)], axis=0
            )
            lat = nn_dot(nope, wkd[j]).astype(BF)
            end = jnp.concatenate([rope.astype(F32), daug], axis=1).astype(BF)
            parts.append(jnp.concatenate([lat, end], axis=1))
        dq = jnp.concatenate(parts, axis=0)
        s = nt_dot(dq, cb[...])
        best = jnp.max(s, axis=1, keepdims=True)
        w = jnp.exp2((s - best) * EXPC)
        total = jnp.sum(w, axis=1, keepdims=True)
        acc = nn_dot(w.astype(BF), cb[:, pl.ds(0, LAT)])
        for j in range(4):
            rest = acc[j * 32 : (j + 1) * 32]
            split = []
            for _ in range(3):
                piece = rest.astype(BF)
                split.append(piece)
                rest = rest - piece.astype(F32)
            y = nn_dot(jnp.concatenate(split, axis=0), wvd[j])
            y = (y[0:32] + y[32:64] + y[64:96]) / total[j * 32 : (j + 1) * 32]
            y = y.astype(BF)
            for t in range(STEPS):
                do_own[t, :, j * VHEAD : (j + 1) * VHEAD] = y[t * DOCS : (t + 1) * DOCS]

    @pl.when(step == DEC + 2)
    def _():
        for off in range(1, NSPAN):
            o_copy(off).wait()
        selo = jnp.where(assign_ref[...] == span * DOCS + iota((DOCS, 128), 0), 1.0, 0.0).astype(BF)
        for t in range(STEPS):
            full = jnp.concatenate([doall[i, t] for i in range(NSPAN)], axis=0)
            so[t] = nn_dot(selo, full).astype(BF)

    @pl.when(step >= NG)
    def _():
        base = (step - NG) * GROUP * TOK
        count = GROUP // CH

        def at(n):
            return pl.ds(pl.multiple_of(base + n * CH * TOK, CH * TOK), CH * TOK)

        def score(n):
            return nt_dot(qa[at(n), :], cb[pl.ds(0, 8 * TOK), :])

        s_next = score(0)
        for n in range(count):
            s = s_next
            if n + 1 < count:
                s_next = score(n + 1)
            s = jnp.concatenate([s, s1[at(n), :]], axis=1)
            best = jnp.max(s, axis=1, keepdims=True)
            w = jnp.exp2((s - best) * EXPC)
            total = jnp.sum(w, axis=1, keepdims=True)
            o = (nn_dot(w.astype(BF), cb[pl.ds(0, 9 * TOK), pl.ds(0, LAT)]) / total).astype(BF)
            for j in range(CH):
                h = n * CH + j
                out_ref[:, h * VHEAD : (h + 1) * VHEAD] = nn_dot(
                    o[j * TOK : (j + 1) * TOK], wv_ref[h]
                ).astype(BF)

    @pl.when(step == DEC)
    def _():
        for off in (1, 7, 2, 6, 3, 5, 4):
            o_copy(off).start()
        doall[span] = do_own[...]

    @pl.when(step == DEC + 2)
    def _():
        for n in (3, 0, 6, 1, 5, 2, 4, 7):
            s_out(n).start()
        columns(me)[...] = so[...]

    @pl.when(step == 2 * NG - 1)
    def _():
        for n in range(7):
            s_landed(n)
            s_out(8 + n).start()
        for n in range(7, 15):
            s_landed(n)
        for n in range(15):
            s_out(n).wait_send()
        dec_ref[...] = outbuf[...]


def body(
    q_prefill, kv_latent, key_rope, segment_ids, assignment, absorb_key, absorb_value,
    q_decode, new_latent, new_rope,
):
    vmem = pl.BlockSpec(memory_space=pltpu.VMEM)
    hbm = pl.BlockSpec(memory_space=pl.ANY)
    out, dec = pl.pallas_call(
        kernel,
        grid=(2 * NG,),
        out_shape=(
            jax.ShapeDtypeStruct((TOK, H * VHEAD), BF),
            jax.ShapeDtypeStruct((STEPS, DOCS, H * VHEAD), BF),
        ),
        in_specs=[vmem] * 7
        + [
            hbm,
            hbm,
            pl.BlockSpec((GROUP, NOPE + ROPE, TOK), lambda i: (jnp.minimum(i, NG - 1), 0, 0)),
            pl.BlockSpec((GROUP, NOPE, LAT), lambda i: (jnp.minimum(i, NG - 1), 0, 0)),
            pl.BlockSpec((GROUP, LAT, VHEAD), lambda i: (jnp.maximum(i - NG, 0), 0, 0)),
        ],
        out_specs=(
            pl.BlockSpec((TOK, GROUP * VHEAD), lambda i: (0, jnp.maximum(i - NG, 0))),
            pl.BlockSpec((STEPS, DOCS, H * VHEAD), lambda i: (0, 0, 0)),
        ),
        scratch_shapes=[
            pltpu.VMEM((17 * TOK, WIDE), BF),
            pltpu.VMEM((H * TOK, WIDE), BF),
            pltpu.VMEM((H * TOK, TOK), F32),
            pltpu.VMEM((AUG, TOK), BF),
            pltpu.VMEM((STEPS, DOCS * 8, NOPE), F32),
            pltpu.VMEM((STEPS, DOCS * 8, NOPE), F32),
            pltpu.VMEM((DOCS, QCOL), BF),
            pltpu.VMEM((NSPAN * DOCS, QCOL), BF),
            pltpu.VMEM((128, 128), F32),
            pltpu.VMEM((4, NOPE, LAT), BF),
            pltpu.VMEM((4, LAT, VHEAD), BF),
            pltpu.VMEM((STEPS, DOCS, 512), BF),
            pltpu.VMEM((NSPAN, STEPS, DOCS, 512), BF),
            pltpu.VMEM((STEPS, DOCS, 512), BF),
            pltpu.VMEM((STEPS, DOCS, H * VHEAD), BF),
            pltpu.SemaphoreType.DMA((15,)),
            pltpu.SemaphoreType.DMA((15,)),
            pltpu.SemaphoreType.DMA((7,)),
            pltpu.SemaphoreType.DMA((7,)),
            pltpu.SemaphoreType.DMA((7,)),
            pltpu.SemaphoreType.DMA((7,)),
            pltpu.SemaphoreType.DMA((15,)),
            pltpu.SemaphoreType.DMA((15,)),
            pltpu.SemaphoreType.DMA((2,)),
        ],
        compiler_params=pltpu.CompilerParams(
            dimension_semantics=("arbitrary",),
            collective_id=0,
            has_side_effects=True,
            vmem_limit_bytes=60 * 1024 * 1024,
        ),
    )(
        kv_latent[0], key_rope[0].T, segment_ids, assignment.reshape(1, 128), q_decode,
        new_latent, new_rope, absorb_key, absorb_value,
        q_prefill[0].transpose(1, 2, 0), absorb_key, absorb_value,
    )
    return (out[None], dec)


def solution(mesh):
    in_specs = (
        P("span", "seq", None, None),
        P("span", "seq", None),
        P("span", "seq", None),
        P(),
        P(),
        P(),
        P(),
        P(None, "span", None, None),
        P(None, "span", None),
        P(None, "span", None),
    )
    out_specs = (P("span", "seq", None), P(None, "span", None))
    return jax.shard_map(body, mesh=mesh, in_specs=in_specs, out_specs=out_specs, check_vma=False)
```

time: 105 us -> 77.5 us (0.74)
  local copies, waits for them, and re-layouts: 18.9 us -> 3.95 us
  other arithmetic: 9.49 us -> 0 us
  Pallas kernels: 74.7 us -> 72.6 us
    unnamed x6 -> x4, local copies, waits for them, and re-layouts: 12.5 us -> 3.95 us
    dynamic_slice x4 -> x0, local copies, waits for them, and re-layouts: 4.6 us -> none  [the longest x1 1.87 us: body(): wvd = lax.dynamic_slice(absorb_value, (me * 4, 0, 0), (4, LAT, VHEAD))]
    convert_element_type x3 -> x0, other arithmetic: 2.85 us -> none  [the longest x1 1.32 us: body(): sel = (own_docs[:, None] == every[None, :]).astype(BF)]
    pallas_call x1, Pallas kernels: 74.7 us -> 72.6 us  [body(): pl.pallas_call(kernel, grid=(2 * NG,), out_shape=(jax.ShapeDtypeStruct((T...]
    concatenate x3 -> x0, other arithmetic: 2.07 us -> none  [the longest x1 0.7 us: cache_rows(): return jnp.concatenate([normed, rope.astype(F32)], axis=-1).astype(BF)]
    another operation x6 -> x0, other arithmetic: 2 us -> none
    reduce_sum x2 -> x0, other arithmetic: 1.86 us -> none  [cache_rows(): jnp.mean(values * values, axis=-1, keepdims=True) + EPS]
where the time goes in v1:
time: 77.5 us; the launch traced here: 77.2 us
  Pallas kernels  72.6 us (94%)
  local copies, waits for them, and re-layouts  3.95 us (5%)
    pallas_call x1, Pallas kernels, body(): pl.pallas_call(kernel, grid=(2 * NG,), out_shape=(jax.ShapeDtypeStruct((T...  72.6 us
    unnamed x4, local copies, waits for them, and re-layouts  3.95 us

profile of v1, /device:TPU:1, one launch (start us, length us, event | category | flops | bytes accessed | tf_op | source)
XLA Modules:
  0.0 77.2 jit_solution(18383678327118761128)
XLA Ops:
  0.6 72.6 %shard_map.113 = (bf16[128,8192]{1,0:T(8,128)(2,1)}, bf16[2,16,8192]{2,1,0:T(8,128)(2,1)}) custom-call(bf16[128,512]{1,0:T(8,128)(2,1)} %bitcast.11, bf16[64,128]{1,0:T(8,128)(2,1)} %bitcast.12, s32[8,2048]{1,0:T(8,128)} %seg_ref.1, s32[1,128]{1,0:T(1,128)} %bitcast.13, bf16[2,16,64,192]{3,2,1,0:T(8,128)(2,1)} %qd_ref.1, bf16[2,16,512]{2,1,0:T(8,128)(2,1)} %nl_ref.1, ...), custom_call_target="tpu_custom_call" | custom-call | tf_op jit(solution)/shard_map/pallas_call | solution.py:439
  73.2 0.0 copy-start
  73.3 3.2 %copy.14 = bf16[1,128,8192]{2,1,0:T(8,128)(2,1)} copy(bf16[1,128,8192]{2,1,0:T(8,128)(2,1)} %bitcast.10) | data formatting | bytes 4194304
  76.4 0.0 copy-done
  76.4 0.8 %copy.15 = bf16[2,16,8192]{2,1,0:T(8,128)(2,1)} copy(bf16[2,16,8192]{2,1,0:T(8,128)(2,1)S(1)} %copy-done) | data formatting | bytes 1048576
Async XLA Ops:
  73.2 3.2 %copy-start = (bf16[2,16,8192]{2,1,0:T(8,128)(2,1)S(1)}, bf16[2,16,8192]{2,1,0:T(8,128)(2,1)}, u32[]{:S(2)}) copy-start(bf16[2,16,8192]{2,1,0:T(8,128)(2,1)} %get-tuple-element.9) | copy-start | bytes 1572868

commit v2 on v1

--- a/solution.py
+++ b/solution.py
@@ -25,10 +25,13 @@
 EXPC = SCALE * math.log2(math.e)
 GROUP = 8
 NG = H // GROUP
-CH = 2
-RELAY0 = 4
-RELAY1 = 6
-DEC = NG + 2
+CH = 4
+RELAY0 = 5
+EARLY = NG
+MIDDLE = NG + 1
+LATE = NG + 2
+DEC = LATE + 2
+LAST = LATE + NG - 1
 QCOL = 2688
 FRESH = 1536
 BF = jnp.bfloat16
@@ -58,7 +61,7 @@
     lat_ref, rope_ref, seg_ref, assign_ref, qd_ref, nl_ref, nr_ref, wk_any, wv_any,
     q_ref, wk_ref, wv_ref,
     out_ref, dec_ref,
-    cb, qa, s1, qaug, qf, qr, qm, qall, selbuf, wkd, wvd, do_own, doall, so, outbuf,
+    cb, qa, s1, s2, s3, qaug, qf, qr, qm, qall, selbuf, wkd, wvd, do_own, doall, so, outbuf,
     g_send, g_recv, q_send, q_recv, o_send, o_recv, s_send, s_recv, w_sem,
 ):
     step = pl.program_id(0)
@@ -79,9 +82,18 @@
     up = idx(zp, yh, k)
     down = idx(zm, yh, k)
 
+    def less(a, b):
+        return (b - a + 31) // 32
+
     def rows(block, owner):
         slot = (block - owner + 24) % 16
-        return cb.at[pl.ds(pl.multiple_of(slot * TOK, TOK), TOK)]
+        phase = owner % 4
+        back = (owner // 4 - block // 4 + 4) % 4
+        near = less(0, back) * less(back, 2)
+        other = (block % 4 // 2 + phase // 2) % 2
+        high = less(7 - phase, slot) * less(slot, 8)
+        place = near * (4 + 2 * other + block % 2) + (1 - near) * (slot - 4 * high)
+        return cb.at[pl.ds(pl.multiple_of(place * TOK, TOK), TOK)]
 
     kinds = [
         idx(z, 1 - yh, k),
@@ -279,14 +291,26 @@
         send(7).start()
         send(8).start()
 
-    @pl.when(step == RELAY1)
+    def early_scores(place, dst):
+        keys = cb[pl.ds(place * TOK, 2 * TOK), :]
+
+        def chunk(n, carry):
+            at = pl.ds(pl.multiple_of(n * 4 * TOK, 4 * TOK), 4 * TOK)
+            dst[at, :] = nt_dot(qa[at, :], keys)
+            return carry
+
+        lax.fori_loop(0, H // 4, chunk, 0)
+
+    @pl.when(step == EARLY)
     def _():
         landed(0)
         for i in (4, 5, 6, 3):
             send(i).start()
         q_send_of(0).start()
-
-    @pl.when(step == NG)
+        landed(9)
+        early_scores(4, s2)
+
+    @pl.when(step == MIDDLE)
     def _():
         landed(3)
         send(9).start()
@@ -295,15 +319,20 @@
         send(11).start()
         landed(5)
         send(13).start()
+        landed(11)
+        early_scores(6, s3)
+
+    @pl.when(step == LATE)
+    def _():
         landed(6)
         send(14).start()
         q_landed(0)
         for n in (4, 6, 5):
             q_send_of(n).start()
-        for kind in (7, 8, 9, 11, 13, 14):
+        for kind in (7, 8, 13, 14):
             landed(kind)
 
-    @pl.when(step == NG + 1)
+    @pl.when(step == LATE + 1)
     def _():
         landed(2)
         send(12).start()
@@ -379,23 +408,23 @@
             full = jnp.concatenate([doall[i, t] for i in range(NSPAN)], axis=0)
             so[t] = nn_dot(selo, full).astype(BF)
 
-    @pl.when(step >= NG)
-    def _():
-        base = (step - NG) * GROUP * TOK
+    @pl.when(step >= LATE)
+    def _():
+        base = (step - LATE) * GROUP * TOK
         count = GROUP // CH
 
         def at(n):
             return pl.ds(pl.multiple_of(base + n * CH * TOK, CH * TOK), CH * TOK)
 
         def score(n):
-            return nt_dot(qa[at(n), :], cb[pl.ds(0, 8 * TOK), :])
+            return nt_dot(qa[at(n), :], cb[pl.ds(0, 4 * TOK), :])
 
         s_next = score(0)
         for n in range(count):
             s = s_next
             if n + 1 < count:
                 s_next = score(n + 1)
-            s = jnp.concatenate([s, s1[at(n), :]], axis=1)
+            s = jnp.concatenate([s, s2[at(n), :], s3[at(n), :], s1[at(n), :]], axis=1)
             best = jnp.max(s, axis=1, keepdims=True)
             w = jnp.exp2((s - best) * EXPC)
             total = jnp.sum(w, axis=1, keepdims=True)
@@ -418,7 +447,7 @@
             s_out(n).start()
         columns(me)[...] = so[...]
 
-    @pl.when(step == 2 * NG - 1)
+    @pl.when(step == LAST)
     def _():
         for n in range(7):
             s_landed(n)
@@ -438,7 +467,7 @@
     hbm = pl.BlockSpec(memory_space=pl.ANY)
     out, dec = pl.pallas_call(
         kernel,
-        grid=(2 * NG,),
+        grid=(LATE + NG,),
         out_shape=(
             jax.ShapeDtypeStruct((TOK, H * VHEAD), BF),
             jax.ShapeDtypeStruct((STEPS, DOCS, H * VHEAD), BF),
@@ -449,16 +478,18 @@
             hbm,
             pl.BlockSpec((GROUP, NOPE + ROPE, TOK), lambda i: (jnp.minimum(i, NG - 1), 0, 0)),
             pl.BlockSpec((GROUP, NOPE, LAT), lambda i: (jnp.minimum(i, NG - 1), 0, 0)),
-            pl.BlockSpec((GROUP, LAT, VHEAD), lambda i: (jnp.maximum(i - NG, 0), 0, 0)),
+            pl.BlockSpec((GROUP, LAT, VHEAD), lambda i: (jnp.maximum(i - LATE, 0), 0, 0)),
         ],
         out_specs=(
-            pl.BlockSpec((TOK, GROUP * VHEAD), lambda i: (0, jnp.maximum(i - NG, 0))),
+            pl.BlockSpec((TOK, GROUP * VHEAD), lambda i: (0, jnp.maximum(i - LATE, 0))),
             pl.BlockSpec((STEPS, DOCS, H * VHEAD), lambda i: (0, 0, 0)),
         ),
         scratch_shapes=[
             pltpu.VMEM((17 * TOK, WIDE), BF),
             pltpu.VMEM((H * TOK, WIDE), BF),
             pltpu.VMEM((H * TOK, TOK), F32),
+            pltpu.VMEM((H * TOK, 2 * TOK), F32),
+            pltpu.VMEM((H * TOK, 2 * TOK), F32),
             pltpu.VMEM((AUG, TOK), BF),
             pltpu.VMEM((STEPS, DOCS * 8, NOPE), F32),
             pltpu.VMEM((STEPS, DOCS * 8, NOPE), F32),

time: 77.5 us -> 74.7 us (0.964)
  Pallas kernels: 72.6 us -> 69.8 us
    pallas_call x1, Pallas kernels: 72.6 us -> 69.8 us  [body(): pl.pallas_call(kernel, grid=(LATE + NG,), out_shape=(jax.ShapeDtypeStruct...]
where the time goes in v2:
time: 74.7 us; the launch traced here: 74.4 us
  Pallas kernels  69.8 us (93%)
  local copies, waits for them, and re-layouts  3.95 us (5%)
    pallas_call x1, Pallas kernels, body(): pl.pallas_call(kernel, grid=(LATE + NG,), out_shape=(jax.ShapeDtypeStruct...  69.8 us
    unnamed x4, local copies, waits for them, and re-layouts  3.95 us

profile of v2, /device:TPU:1, one launch (start us, length us, event | category | flops | bytes accessed | tf_op | source)
XLA Modules:
  0.0 74.4 jit_solution(5432341064245023721)
XLA Ops:
  0.6 69.8 %shard_map.113 = (bf16[128,8192]{1,0:T(8,128)(2,1)}, bf16[2,16,8192]{2,1,0:T(8,128)(2,1)}) custom-call(bf16[128,512]{1,0:T(8,128)(2,1)} %bitcast.11, bf16[64,128]{1,0:T(8,128)(2,1)} %bitcast.12, s32[8,2048]{1,0:T(8,128)} %seg_ref.1, s32[1,128]{1,0:T(1,128)} %bitcast.13, bf16[2,16,64,192]{3,2,1,0:T(8,128)(2,1)} %qd_ref.1, bf16[2,16,512]{2,1,0:T(8,128)(2,1)} %nl_ref.1, ...), custom_call_target="tpu_custom_call" | custom-call | tf_op jit(solution)/shard_map/pallas_call | solution.py:468
  70.5 0.0 copy-start
  70.5 3.2 %copy.14 = bf16[1,128,8192]{2,1,0:T(8,128)(2,1)} copy(bf16[1,128,8192]{2,1,0:T(8,128)(2,1)} %bitcast.10) | data formatting | bytes 4194304
  73.6 0.0 copy-done
  73.6 0.8 %copy.15 = bf16[2,16,8192]{2,1,0:T(8,128)(2,1)} copy(bf16[2,16,8192]{2,1,0:T(8,128)(2,1)S(1)} %copy-done) | data formatting | bytes 1048576
Async XLA Ops:
  70.5 3.2 %copy-start = (bf16[2,16,8192]{2,1,0:T(8,128)(2,1)S(1)}, bf16[2,16,8192]{2,1,0:T(8,128)(2,1)}, u32[]{:S(2)}) copy-start(bf16[2,16,8192]{2,1,0:T(8,128)(2,1)} %get-tuple-element.9) | copy-start | bytes 1572868

commit v3 on v2

--- a/solution.py
+++ b/solution.py
@@ -30,7 +30,7 @@
 EARLY = NG
 MIDDLE = NG + 1
 LATE = NG + 2
-DEC = LATE + 2
+DEC = LATE + 1
 LAST = LATE + NG - 1
 QCOL = 2688
 FRESH = 1536
@@ -299,7 +299,7 @@
             dst[at, :] = nt_dot(qa[at, :], keys)
             return carry
 
-        lax.fori_loop(0, H // 4, chunk, 0)
+        lax.fori_loop(0, H // 4, chunk, 0, unroll=4)
 
     @pl.when(step == EARLY)
     def _():
@@ -319,23 +319,20 @@
         send(11).start()
         landed(5)
         send(13).start()
-        landed(11)
-        early_scores(6, s3)
-
-    @pl.when(step == LATE)
-    def _():
-        landed(6)
-        send(14).start()
         q_landed(0)
         for n in (4, 6, 5):
             q_send_of(n).start()
+        landed(11)
+        early_scores(6, s3)
+
+    @pl.when(step == LATE)
+    def _():
+        landed(6)
+        send(14).start()
+        landed(2)
+        send(12).start()
         for kind in (7, 8, 13, 14):
             landed(kind)
-
-    @pl.when(step == LATE + 1)
-    def _():
-        landed(2)
-        send(12).start()
 
     @pl.when(step == DEC)
     def _():
@@ -408,6 +405,12 @@
             full = jnp.concatenate([doall[i, t] for i in range(NSPAN)], axis=0)
             so[t] = nn_dot(selo, full).astype(BF)
 
+    @pl.when(step == LAST)
+    def _():
+        for n in range(7):
+            s_landed(n)
+            s_out(8 + n).start()
+
     @pl.when(step >= LATE)
     def _():
         base = (step - LATE) * GROUP * TOK
@@ -449,9 +452,6 @@
 
     @pl.when(step == LAST)
     def _():
-        for n in range(7):
-            s_landed(n)
-            s_out(8 + n).start()
         for n in range(7, 15):
             s_landed(n)
         for n in range(15):

time: 74.7 us -> 70.6 us (0.945)
  Pallas kernels: 69.8 us -> 65.8 us
    pallas_call x1, Pallas kernels: 69.8 us -> 65.8 us  [body(): pl.pallas_call(kernel, grid=(LATE + NG,), out_shape=(jax.ShapeDtypeStruct...]
where the time goes in v3:
time: 70.6 us; the launch traced here: 70.4 us
  Pallas kernels  65.8 us (93%)
  local copies, waits for them, and re-layouts  3.95 us (6%)
    pallas_call x1, Pallas kernels, body(): pl.pallas_call(kernel, grid=(LATE + NG,), out_shape=(jax.ShapeDtypeStruct...  65.8 us
    unnamed x4, local copies, waits for them, and re-layouts  3.95 us

profile of v3, /device:TPU:1, one launch (start us, length us, event | category | flops | bytes accessed | tf_op | source)
XLA Modules:
  0.0 70.4 jit_solution(16864486786655862670)
XLA Ops:
  0.6 65.8 %shard_map.113 = (bf16[128,8192]{1,0:T(8,128)(2,1)}, bf16[2,16,8192]{2,1,0:T(8,128)(2,1)}) custom-call(bf16[128,512]{1,0:T(8,128)(2,1)} %bitcast.11, bf16[64,128]{1,0:T(8,128)(2,1)} %bitcast.12, s32[8,2048]{1,0:T(8,128)} %seg_ref.1, s32[1,128]{1,0:T(1,128)} %bitcast.13, bf16[2,16,64,192]{3,2,1,0:T(8,128)(2,1)} %qd_ref.1, bf16[2,16,512]{2,1,0:T(8,128)(2,1)} %nl_ref.1, ...), custom_call_target="tpu_custom_call" | custom-call | tf_op jit(solution)/shard_map/pallas_call | solution.py:468
  66.4 0.0 copy-start
  66.4 3.2 %copy.14 = bf16[1,128,8192]{2,1,0:T(8,128)(2,1)} copy(bf16[1,128,8192]{2,1,0:T(8,128)(2,1)} %bitcast.10) | data formatting | bytes 4194304
  69.6 0.0 copy-done
  69.6 0.8 %copy.15 = bf16[2,16,8192]{2,1,0:T(8,128)(2,1)} copy(bf16[2,16,8192]{2,1,0:T(8,128)(2,1)S(1)} %copy-done) | data formatting | bytes 1048576
Async XLA Ops:
  66.4 3.2 %copy-start = (bf16[2,16,8192]{2,1,0:T(8,128)(2,1)S(1)}, bf16[2,16,8192]{2,1,0:T(8,128)(2,1)}, u32[]{:S(2)}) copy-start(bf16[2,16,8192]{2,1,0:T(8,128)(2,1)} %get-tuple-element.9) | copy-start | bytes 1572868

commit v4 on v3

--- a/solution.py
+++ b/solution.py
@@ -13,6 +13,7 @@
 LAT = 512
 VHEAD = 128
 TOK = 128
+HALF = 64
 DOCS = 16
 STEPS = 2
 NSEQ = 16
@@ -85,7 +86,7 @@
     def less(a, b):
         return (b - a + 31) // 32
 
-    def rows(block, owner):
+    def rows(block, owner, half):
         slot = (block - owner + 24) % 16
         phase = owner % 4
         back = (owner // 4 - block // 4 + 4) % 4
@@ -93,7 +94,7 @@
         other = (block % 4 // 2 + phase // 2) % 2
         high = less(7 - phase, slot) * less(slot, 8)
         place = near * (4 + 2 * other + block % 2) + (1 - near) * (slot - 4 * high)
-        return cb.at[pl.ds(pl.multiple_of(place * TOK, TOK), TOK)]
+        return cb.at[pl.ds(pl.multiple_of(place * TOK + half * HALF, HALF), HALF)]
 
     kinds = [
         idx(z, 1 - yh, k),
@@ -106,12 +107,12 @@
     ]
     arrive = kinds + [part] + [b + 1 - 2 * k for b in kinds]
 
-    def copy(src, dst, target, kind, number):
+    def copy(src, dst, target, kind, number, half):
         return pltpu.make_async_remote_copy(
             src_ref=src,
             dst_ref=dst,
-            send_sem=g_send.at[number],
-            recv_sem=g_recv.at[kind],
+            send_sem=g_send.at[2 * number + half],
+            recv_sem=g_recv.at[2 * kind + half],
             device_id=(target, span),
             device_id_type=MESH,
         )
@@ -134,13 +135,19 @@
         (kinds[6], part, 14),
     ]
 
-    def send(i):
+    def send(i, half):
         block, target, kind = plan[i]
-        return copy(rows(block, me), rows(block, target), target, kind, i)
-
-    def landed(kind):
-        dst = rows(arrive[kind], me)
-        copy(dst, dst, part, kind, 0).wait_recv()
+        return copy(rows(block, me, half), rows(block, target, half), target, kind, i, half)
+
+    def go(*numbers, halves=(0, 1)):
+        for half in halves:
+            for i in numbers:
+                send(i, half).start()
+
+    def landed(kind, halves=(0, 1)):
+        for half in halves:
+            dst = rows(arrive[kind], me, half)
+            copy(dst, dst, part, kind, 0, half).wait_recv()
 
     x = span // 2
     lo = span % 2
@@ -264,8 +271,7 @@
         both = jnp.concatenate([nr_ref[0].astype(F32), nr_ref[1].astype(F32)], axis=1)
         qm[:, FRESH + 2 * LAT : QCOL] = both.astype(BF)
         pl.semaphore_wait(barrier, NSEQ + NSPAN - 2)
-        for i in (1, 0, 2):
-            send(i).start()
+        go(1, 0, 2)
         for n in (1, 3, 2):
             q_send_of(n).start()
         qrows(span)[...] = qm[...]
@@ -288,8 +294,7 @@
     @pl.when(step == RELAY0)
     def _():
         landed(1)
-        send(7).start()
-        send(8).start()
+        go(7, 8)
 
     def early_scores(place, dst):
         keys = cb[pl.ds(place * TOK, 2 * TOK), :]
@@ -303,22 +308,24 @@
 
     @pl.when(step == EARLY)
     def _():
-        landed(0)
-        for i in (4, 5, 6, 3):
-            send(i).start()
-        q_send_of(0).start()
+        landed(0, (0,))
+        go(4, 5, 6, halves=(0,))
         landed(9)
         early_scores(4, s2)
+        landed(0, (1,))
+        go(4, 5, 6, halves=(1,))
+        go(3)
+        q_send_of(0).start()
 
     @pl.when(step == MIDDLE)
     def _():
-        landed(3)
-        send(9).start()
-        landed(4)
-        send(10).start()
-        send(11).start()
+        for half in (0, 1):
+            landed(4, (half,))
+            go(10, 11, halves=(half,))
+            landed(3, (half,))
+            go(9, halves=(half,))
         landed(5)
-        send(13).start()
+        go(13)
         q_landed(0)
         for n in (4, 6, 5):
             q_send_of(n).start()
@@ -327,10 +334,11 @@
 
     @pl.when(step == LATE)
     def _():
-        landed(6)
-        send(14).start()
+        for half in (0, 1):
+            landed(6, (half,))
+            go(14, halves=(half,))
         landed(2)
-        send(12).start()
+        go(12)
         for kind in (7, 8, 13, 14):
             landed(kind)
 
@@ -339,7 +347,8 @@
         landed(10)
         landed(12)
         for i in range(15):
-            send(i).wait_send()
+            for half in (0, 1):
+                send(i, half).wait_send()
         wk_copy().wait()
         wv_copy().wait()
         for n in range(1, 7):
@@ -502,8 +511,8 @@
             pltpu.VMEM((NSPAN, STEPS, DOCS, 512), BF),
             pltpu.VMEM((STEPS, DOCS, 512), BF),
             pltpu.VMEM((STEPS, DOCS, H * VHEAD), BF),
-            pltpu.SemaphoreType.DMA((15,)),
-            pltpu.SemaphoreType.DMA((15,)),
+            pltpu.SemaphoreType.DMA((30,)),
+            pltpu.SemaphoreType.DMA((30,)),
             pltpu.SemaphoreType.DMA((7,)),
             pltpu.SemaphoreType.DMA((7,)),
             pltpu.SemaphoreType.DMA((7,)),

time: 70.6 us -> 73.7 us (1.044)
  Pallas kernels: 65.8 us -> 68.8 us
    pallas_call x1, Pallas kernels: 65.8 us -> 68.8 us  [body(): pl.pallas_call(kernel, grid=(LATE + NG,), out_shape=(jax.ShapeDtypeStruct...]
where the time goes in v4:
time: 73.7 us; the launch traced here: 73.4 us
  Pallas kernels  68.8 us (93%)
  local copies, waits for them, and re-layouts  3.95 us (5%)
    pallas_call x1, Pallas kernels, body(): pl.pallas_call(kernel, grid=(LATE + NG,), out_shape=(jax.ShapeDtypeStruct...  68.8 us
    unnamed x4, local copies, waits for them, and re-layouts  3.95 us

profile of v4, /device:TPU:1, one launch (start us, length us, event | category | flops | bytes accessed | tf_op | source)
XLA Modules:
  0.0 73.4 jit_solution(7704699827293546803)
XLA Ops:
  0.6 68.8 %shard_map.113 = (bf16[128,8192]{1,0:T(8,128)(2,1)}, bf16[2,16,8192]{2,1,0:T(8,128)(2,1)}) custom-call(bf16[128,512]{1,0:T(8,128)(2,1)} %bitcast.11, bf16[64,128]{1,0:T(8,128)(2,1)} %bitcast.12, s32[8,2048]{1,0:T(8,128)} %seg_ref.1, s32[1,128]{1,0:T(1,128)} %bitcast.13, bf16[2,16,64,192]{3,2,1,0:T(8,128)(2,1)} %qd_ref.1, bf16[2,16,512]{2,1,0:T(8,128)(2,1)} %nl_ref.1, ...), custom_call_target="tpu_custom_call" | custom-call | tf_op jit(solution)/shard_map/pallas_call | solution.py:477
  69.5 0.0 copy-start
  69.5 3.2 %copy.14 = bf16[1,128,8192]{2,1,0:T(8,128)(2,1)} copy(bf16[1,128,8192]{2,1,0:T(8,128)(2,1)} %bitcast.10) | data formatting | bytes 4194304
  72.7 0.0 copy-done
  72.7 0.8 %copy.15 = bf16[2,16,8192]{2,1,0:T(8,128)(2,1)} copy(bf16[2,16,8192]{2,1,0:T(8,128)(2,1)S(1)} %copy-done) | data formatting | bytes 1048576
Async XLA Ops:
  69.5 3.2 %copy-start = (bf16[2,16,8192]{2,1,0:T(8,128)(2,1)S(1)}, bf16[2,16,8192]{2,1,0:T(8,128)(2,1)}, u32[]{:S(2)}) copy-start(bf16[2,16,8192]{2,1,0:T(8,128)(2,1)} %get-tuple-element.9) | copy-start | bytes 1572868
